TPU v7x, 32 devices: a whole 2x2x4 slice. The times are simulated.
32 devices in a mesh: seq: 8 (over z, y), head: 4 (over x, core).
Axes of the slice: x: 2, y: 2, z: 4, core: 2. Of those that a mesh axis runs over, the one named last changes fastest.
Arguments:
- layer_in: bfloat16 [4096, 2048], P('seq', 'head'), may hold values from -6 to 6
- query_weight: bfloat16 [2048, 1024], P(None, 'head'), may hold values from -0.125 to 0.125
- key_weight: bfloat16 [2048, 1024], P(None, 'head'), may hold values from -0.125 to 0.125
- value_weight: bfloat16 [2048, 1024], P(None, 'head'), may hold values from -0.125 to 0.125
- gate_weight: bfloat16 [2048, 1024], P(None, 'head'), may hold values from -0.125 to 0.125
- beta_weight: bfloat16 [2048, 8], P(None, 'head'), may hold values from -0.125 to 0.125
- decay_weight: bfloat16 [2048, 8], P(None, 'head'), may hold values from -0.125 to 0.125
- conv_weight: float32 [4, 3, 1024], P(None, None, 'head'), may hold values from -3 to 3
- decay_log: float32 [8], P('head'), as said below
- beta_bias: float32 [8], P('head'), as said below
- decay_bias: float32 [8], P('head'), may hold values from -1 to 1
- norm_gain: float32 [128], replicated, may hold values from 0.1 to 1.9
- out_weight: bfloat16 [1024, 2048], P('head'), may hold values from -0.1875 to 0.1875
Outputs:
- layer_out: bfloat16 [4096, 2048], P('seq', 'head')
Inputs may be any that keep to these rules, and one draw needn't show every extreme that they name: decay_log lies between log(0.1 / 4096) and log(0.05). beta_bias lies between log(0.5 * 128 / 4096) and 1.
All inputs are finite; a program needn't handle non-finite values.
Results may differ from a plain program's by a relative error of at most 0.0049.
Values may be sent and summed in bfloat16 or wider, within the bound.
No kernel may reach another device: no remote copies, remote signals or barrier semaphores. Data moves between devices by JAX's collectives and lax.ppermute only.
A program may use at most 128 MiB of HBM per device.

v0:
```python
import jax
import jax.numpy as jnp
from jax import lax
from jax.sharding import PartitionSpec as P

BLOCK = 128
exact_mode = lax.Precision.HIGHEST
norm_floor = 0.0001


def passed_along(value, axis, steps):
    count = lax.axis_size(axis)
    leading, last = (max(0, -steps), min(count, count - steps))
    return lax.ppermute(value, axis, [(source, source + steps) for source in range(leading, last)])


def causal_conv(values, earlier, kernel):
    reach_back = kernel.shape[0] - 1
    tokens = values.shape[0]
    extended = jnp.concatenate([earlier, values], axis=0)
    summed = kernel[0] * values
    for offset in range(1, reach_back + 1):
        summed = (
            summed + kernel[offset] * extended[reach_back - offset : reach_back - offset + tokens]
        )
    return jax.nn.silu(summed)


def unit_rows(values):
    return values * lax.rsqrt(jnp.sum(values * values, axis=-1, keepdims=True) + 1.0)


def unit_lower_inverse(system):
    length = system.shape[-1]
    row_index = lax.broadcasted_iota(jnp.int32, (length, length), 0)
    col_index = lax.broadcasted_iota(jnp.int32, (length, length), 1)
    inverse = jnp.broadcast_to(jnp.eye(length, dtype=jnp.float32), system.shape)
    width = 1
    while width < length:
        same_pair = row_index // (2 * width) == col_index // (2 * width)
        lower_half = row_index // width > col_index // width
        linking = jnp.where(same_pair & lower_half, system, 0.0)
        middle = lax.optimization_barrier(
            jnp.einsum("...rs,...st->...rt", linking, inverse, precision=exact_mode)
        )
        update = lax.optimization_barrier(
            jnp.einsum("...rs,...st->...rt", inverse, middle, precision=exact_mode)
        )
        inverse = inverse - update
        width = width * 2
    return inverse


def block_terms(queries, key_rows, values, beta_gate, log_decay):
    length = log_decay.shape[-1]
    running = jnp.cumsum(log_decay, axis=-1)
    row_index = lax.broadcasted_iota(jnp.int32, (length, length), 0)
    col_index = lax.broadcasted_iota(jnp.int32, (length, length), 1)
    within = row_index >= col_index
    before = row_index > col_index
    spread = running[..., :, None] - running[..., None, :]
    decay_matrix = jnp.where(within, jnp.exp(jnp.minimum(spread, 0.0)), 0.0)
    key_gram = jnp.einsum("...rd,...sd->...rs", key_rows, key_rows, precision=exact_mode)
    lower_part = jnp.where(before, beta_gate[..., :, None] * decay_matrix * key_gram, 0.0)
    system = lower_part + jnp.eye(length, dtype=jnp.float32)
    growth = jnp.exp(running)
    right_side = jnp.concatenate(
        [beta_gate[..., None] * values, (beta_gate * growth)[..., None] * key_rows], axis=-1
    )
    solved = jnp.einsum(
        "...rs,...se->...re", unit_lower_inverse(system), right_side, precision=exact_mode
    )
    value_dim = values.shape[-1]
    fixed_rows = solved[..., :value_dim]
    erased = solved[..., value_dim:]
    query_key = jnp.einsum("...rd,...sd->...rs", queries, key_rows, precision=exact_mode)
    mixing = jnp.where(within, decay_matrix * query_key, 0.0)
    local_out = jnp.einsum("...rs,...se->...re", mixing, fixed_rows, precision=exact_mode)
    removed = lax.optimization_barrier(
        jnp.einsum("...rs,...sd->...rd", mixing, erased, precision=exact_mode)
    )
    reader = growth[..., None] * queries - removed
    tail_decay = jnp.exp(running[..., -1:] - running)
    weighted = tail_decay[..., None] * key_rows
    key_dim = key_rows.shape[-1]
    lost_part = lax.optimization_barrier(
        jnp.einsum("...bd,...be->...de", weighted, erased, precision=exact_mode)
    )
    transit = (
        jnp.exp(running[..., -1])[..., None, None] * jnp.eye(key_dim, dtype=jnp.float32) - lost_part
    )
    carried = jnp.einsum("...bd,...be->...de", weighted, fixed_rows, precision=exact_mode)
    return (local_out, reader, transit, carried)


def compose(earlier, later_map):
    joined = jnp.einsum("...de,...ef->...df", later_map[0], earlier[0], precision=exact_mode)
    moved = (
        jnp.einsum("...de,...ef->...df", later_map[0], earlier[1], precision=exact_mode)
        + later_map[1]
    )
    return (joined, moved)


def on_device(
    layer_in,
    query_weight,
    key_weight,
    value_weight,
    gate_weight,
    beta_weight,
    decay_weight,
    conv_weight,
    decay_log,
    beta_bias,
    decay_bias,
    norm_gain,
    out_weight,
):
    tokens = layer_in.shape[0]
    head_count = beta_weight.shape[1]
    head_dim = query_weight.shape[1] // head_count
    weights = (query_weight, key_weight, value_weight, gate_weight, beta_weight, decay_weight)
    shard_piece = lax.all_gather(layer_in, "head", axis=1, tiled=True)
    query_raw, key_raw, value_raw, gate_raw, beta_raw, decay_raw = tuple(
        (jnp.dot(shard_piece, weight, preferred_element_type=jnp.float32) for weight in weights)
    )
    reach_back = conv_weight.shape[0] - 1
    channels = query_raw.shape[1]
    last_rows = jnp.concatenate(
        [
            query_raw[tokens - reach_back :],
            key_raw[tokens - reach_back :],
            value_raw[tokens - reach_back :],
        ],
        axis=1,
    )
    prior_rows = passed_along(last_rows, "seq", 1)
    mixed_query = causal_conv(query_raw, prior_rows[:, :channels], conv_weight[:, 0])
    mixed_key = causal_conv(key_raw, prior_rows[:, channels : 2 * channels], conv_weight[:, 1])
    mixed_value = causal_conv(value_raw, prior_rows[:, 2 * channels :], conv_weight[:, 2])
    queries = unit_rows(mixed_query.reshape(tokens, head_count, head_dim))
    key_rows = unit_rows(mixed_key.reshape(tokens, head_count, head_dim))
    values = mixed_value.reshape(tokens, head_count, head_dim)
    beta_gate = jax.nn.sigmoid(beta_raw + beta_bias)
    log_decay = -jnp.exp(decay_log) * jax.nn.softplus(decay_raw + decay_bias)
    blocks = tokens // BLOCK

    def arrange(array):
        return array.reshape(blocks, BLOCK, head_count, head_dim).transpose(0, 2, 1, 3)

    def arrange_gate(array):
        return array.reshape(blocks, BLOCK, head_count).transpose(0, 2, 1)

    local_out, reader, transit, carried = block_terms(
        arrange(queries),
        arrange(key_rows),
        arrange(values),
        arrange_gate(beta_gate),
        arrange_gate(log_decay),
    )
    identity = jnp.broadcast_to(
        jnp.eye(head_dim, dtype=jnp.float32), (head_count, head_dim, head_dim)
    )
    nothing = jnp.zeros((head_count, head_dim, head_dim), jnp.float32)

    def through(running_pair, block_maps):
        return (compose(running_pair, block_maps), None)

    slab_pair, unused_rest = lax.scan(through, (identity, nothing), (transit, carried))
    slab_transit, slab_state = slab_pair
    stacked = jnp.stack([slab_transit, slab_state], axis=0)[None]
    every_map = lax.all_gather(stacked, "seq", axis=0, tiled=True)
    every_transit = every_map[:, 0]
    every_state = every_map[:, 1]
    position = lax.axis_index("seq")
    order = lax.broadcasted_iota(jnp.int32, (every_transit.shape[0], 1, 1, 1), 0)
    earlier_ones = order < position
    affine = (
        jnp.where(earlier_ones, every_transit, identity[None]),
        jnp.where(earlier_ones, every_state, 0.0),
    )
    while affine[0].shape[0] > 1:
        affine = compose((affine[0][0::2], affine[1][0::2]), (affine[0][1::2], affine[1][1::2]))
    incoming = affine[1][0]

    def advance(carry_state, block_maps):
        following = (
            jnp.einsum("hde,hef->hdf", block_maps[0], carry_state, precision=exact_mode)
            + block_maps[1]
        )
        return (following, carry_state)

    unused_last, starts = lax.scan(advance, incoming, (transit, carried))
    outputs = local_out + jnp.einsum("nhrd,nhde->nhre", reader, starts, precision=exact_mode)
    head_out = outputs.transpose(0, 2, 1, 3).reshape(tokens, head_count, head_dim)
    gate_rows = gate_raw.reshape(tokens, head_count, head_dim)
    scaled = head_out * lax.rsqrt(
        jnp.mean(head_out * head_out, axis=-1, keepdims=True) + norm_floor
    )
    hidden = (
        (scaled * norm_gain * jax.nn.silu(gate_rows))
        .reshape(tokens, head_count * head_dim)
        .astype(jnp.bfloat16)
    )
    column_weight = lax.all_to_all(out_weight, "head", split_axis=1, concat_axis=0, tiled=True)
    summed = jnp.dot(
        lax.all_gather(hidden, "head", axis=1, tiled=True),
        column_weight,
        preferred_element_type=jnp.float32,
    )
    return summed.astype(jnp.bfloat16)


def solution(mesh):
    return jax.shard_map(
        on_device,
        mesh=mesh,
        in_specs=(
            P("seq", "head"),
            P(None, "head"),
            P(None, "head"),
            P(None, "head"),
            P(None, "head"),
            P(None, "head"),
            P(None, "head"),
            P(None, None, "head"),
            P("head"),
            P("head"),
            P("head"),
            P(),
            P("head", None),
        ),
        out_specs=P("seq", "head"),
        check_vma=False,
    )
```

profile of v0, /device:TPU:0, one launch (start us, length us, event | category | flops | bytes accessed | tf_op | source)
XLA Modules:
  0.0 182.9 jit_solution(447879425216133817)
XLA Ops:
  7.5 1.2 exponential_negate_fusion
  8.7 1.5 fusion.147
  10.7 23.5 %all-gather.5.cloned.1.call-done = bf16[512,2048]{1,0:T(8,128)(2,1)} async-done(((bf16[512,512]{1,0:T(8,128)(2,1)}), bf16[512,2048]{1,0:T(8,128)(2,1)}) %all-gather.5.cloned.1.call-update) | async-done | bytes 2097168 | tf_op jit(solution)/shard_map/all_gather | solution.py:124
  34.2 2.4 %fusion.135 = f32[4,2,128]{2,1,0:T(2,128)S(1)} fusion(bf16[512,2048]{1,0:T(8,128)(2,1)} %all-gather.5.cloned.1.call-done, bf16[2048,2]{0,1:T(2,128)(2,1)} %param.23, f32[2]{0:T(128)} %param.27, f32[2]{0:T(128)} %exponential_negate_fusion), kind=kOutput, calls=%fused_computation.194 | convolution fusion | flops 4202496 | bytes 2109456 | tf_op jit(solution)/shard_map/dot_general | solution.py:126
  36.7 1.2 reduce_window_sum.11
  41.7 3.6 %collective-permute-start = (f32[3,768]{1,0:T(4,128)S(1)}, f32[3,768]{1,0:T(4,128)S(1)}, u32[]{:S(2)}, u32[]{:S(2)}) collective-permute-start(f32[3,768]{1,0:T(4,128)S(1)} %pad_maximum_fusion.4), channel_id=1, source_target_pairs={{0,4},{4,8},{8,12},{12,16},{16,20},{20,24},{24,28},{1,5},{5,9},{9,... | collective-permute-start | bytes 27656 | tf_op jit(solution)/shard_map/ppermute | solution.py:14
  46.5 2.2 %fusion.146 = (f32[512,256]{1,0:T(8,128)S(1)}, f32[512,256]{1,0:T(8,128)S(1)}) fusion(f32[512,256]{1,0:T(8,128)} %copy-done.7, f32[3,256]{1,0:T(4,128)S(1)} %get-tuple-element.120, f32[256]{0:T(256)} %bitcast.193, f32[256]{0:T(256)} %bitcast.194, f32[256]{0:T(256)} %bitcast.195, f32[256]{0:T(256)} %bitcast.196), kind=kLoop, calls=%fused_computation.241 | loop fusion | flops 1966080 | bytes 1580032 | tf_op jit(solution)/shard_map/mul | solution.py:30
  50.0 1.4 fusion.16
  60.5 1.4 fusion.157
  63.2 1.6 fusion.145
  65.3 2.2 %fusion.27 = f32[4,2,128,256]{3,2,1,0:T(8,128)S(1)} fusion(f32[4,2,128,128]{3,2,1,0:T(8,128)} %bitcast_multiply_fusion.3, f32[4,2,128,128]{3,2,1,0:T(8,128)S(1)} %bitcast_multiply_fusion.1, f32[4,2,128,128]{3,2,1,0:T(8,128)S(1)} %sub.166, f32[4,2,128,128]{3,2,1,0:T(8,128)} %fusion.157), kind=kOutput, calls=%fused_computation.42 | convolution fusion | flops 403046400 | bytes 3145728 | tf_op jit(solution)/shard_map/...rs,...se->...re/dot_general | solution.py:70
  67.5 2.1 %fusion.81 = f32[4,2,128,128]{3,2,1,0:T(8,128)} fusion(f32[4,2,128,256]{3,2,1,0:T(8,128)S(1)} %fusion.27, f32[4,128,2,128]{3,2,1,0:T(2,128)S(1)} %reshape.141, f32[4,2,128]{2,1,0:T(2,128)S(1)} %get-tuple-element.124, f32[4,128,2]{1,2,0:T(2,128)S(1)} %bitcast.179), kind=kOutput, calls=%fused_computation.117 | convolution fusion | flops 201588736 | bytes 1581056 | tf_op jit(solution)/shard_map/...bd,...be->...de/dot_general | solution.py:92
  69.6 1.3 fusion.82
  71.0 6.0 %while.28 = (s32[]{:T(128)}, f32[2,128,128]{2,1,0:T(8,128)S(1)}, f32[2,128,128]{2,1,0:T(8,128)S(1)}, f32[4,2,128,128]{3,2,1,0:T(8,128)S(1)}, f32[4,2,128,128]{3,2,1,0:T(8,128)}) while((s32[]{:T(128)}, f32[2,128,128]{2,1,0:T(8,128)S(1)}, f32[2,128,128]{2,1,0:T(8,128)S(1)}, f32[4,2,128,128]{3,2,1,0:T(8,128)S(1)}, ...), condition=%wide.region_4.5_spmd.clone.clone, body=%wide.region_3.4_spmd.clone.sunk.clone | while | flops 100728832 | bytes 1443410 | solution.py:170
  72.6 1.2 convolution_add_fusion.12
  75.6 1.2 convolution_add_fusion.12
  77.9 2.1 %mul.279 = f32[512,2,128]{2,1,0:T(2,128)} reshape(f32[512,256]{1,0:T(8,128)} %get-tuple-element.101) | data formatting | bytes 1048576 | tf_op jit(solution)/shard_map/mul | solution.py:30
  80.0 2.4 %reduce_sum.27 = f32[512,2]{1,0:T(8,128)} reduce(f32[512,2,128]{2,1,0:T(2,128)} %mul.279, f32[]{:T(128)} %constant.223.clone.1), dimensions={2}, to_apply=%region_1.2 | reduce | flops 130048 | bytes 528388 | tf_op jit(solution)/shard_map/reduce_sum | solution.py:30
  82.4 1.7 add_rsqrt_fusion.1
  85.2 2.1 %reshape.140 = f32[4,128,2,128]{3,2,1,0:T(2,128)} reshape(f32[512,256]{1,0:T(8,128)} %get-tuple-element.102) | data formatting | bytes 1048576 | tf_op jit(solution)/shard_map/reshape | solution.py:142
  87.3 2.4 %fusion.17 = f32[4,2,128,128]{3,2,1,0:T(8,128)S(1)} fusion(f32[4,128,2,128]{3,2,1,0:T(2,128)} %reshape.140, f32[4,128,2,128]{3,2,1,0:T(2,128)S(1)} %reshape.141, f32[4,128,2]{1,2,0:T(2,128)S(1)} %bitcast.181, f32[4,128,2]{1,2,0:T(2,128)S(1)} %bitcast.182, f32[4,2,128]{2,1,0:T(2,128)S(1)} %reduce_window_sum.11, pred[128,128]{1,0:T(8,128)(4,1)S(1)} %get-tuple-element.137), kind=kOutput, calls=%fused_computation.25 | convolution fusion | flops 202244096 | bytes 1601536 | tf_op jit(solution)/shard_map/...rd,...sd->...rs/dot_general | solution.py:76
  89.7 1.5 fusion.84
  91.2 1.8 fusion.87
  92.9 35.0 %all-gather.9.cloned.1.call-done = f32[16,2,128,128]{3,2,1,0:T(8,128)} async-done(((f32[2,2,128,128]{3,2,1,0:T(8,128)}), f32[16,2,128,128]{3,2,1,0:T(8,128)}) %all-gather.9.cloned.1.call-update) | async-done | bytes 2097168 | tf_op jit(solution)/shard_map/all_gather | solution.py:173
  127.9 1.8 %fusion.25 = (f32[8,2,128,128]{3,2,1,0:T(8,128)S(1)}, f32[8,2,128,128]{3,2,1,0:T(8,128)S(1)}) fusion(f32[8,2,2,128,128]{4,3,2,1,0:T(8,128)} %bitcast.173, pred[8]{0:T(512)(128)(4,1)S(1)} %iota_compare_fusion.3, f32[128,128]{1,0:T(8,128)S(1)} %fusion.133), kind=kLoop, calls=%fused_computation.39 | loop fusion | flops 524288 | bytes 4259848 | tf_op jit(solution)/shard_map/jit(_where)/select_n | solution.py:181
  132.0 7.5 %while.27 = (s32[]{:T(128)}, f32[2,128,128]{2,1,0:T(8,128)S(1)}, f32[4,2,128,128]{3,2,1,0:T(8,128)}, f32[4,2,128,128]{3,2,1,0:T(8,128)S(1)}, f32[4,2,128,128]{3,2,1,0:T(8,128)}) while((s32[]{:T(128)}, f32[2,128,128]{2,1,0:T(8,128)S(1)}, f32[4,2,128,128]{3,2,1,0:T(8,128)}, f32[4,2,128,128]{3,2,1,0:T(8,128)S(1)}, ...), condition=%wide.region_6.7_spmd.clone, body=%wide.region_5.6_spmd.sunk.clone | while | flops 50364416 | bytes 1049673 | solution.py:194
  139.6 3.8 %multiply_reduce_fusion = (f32[4,128,2]{1,2,0:T(2,128)S(1)}, f32[4,128,2,128]{1,3,2,0:T(8,128)}) fusion(f32[4,2,128,128]{2,3,1,0:T(8,128)} %fusion.87, f32[4,2,128,128]{3,2,1,0:T(8,128)} %get-tuple-element.62, f32[4,2,128,128]{3,2,1,0:T(8,128)} %fusion.84, f32[4,128,2,128]{3,2,1,0:T(2,128)} %reshape.140, f32[4,2,128]{2,1,0:T(2,128)S(1)} %get-tuple-element.122, ...), kind=kOutput, calls=%fused_computation.93 | convolution fusion | flops 202112000 | bytes 2633728 | tf_op jit(solution)/shard_map/nhrd,nhde->nhre/dot_general | solution.py:195
  143.5 2.0 %copy.104 = f32[4,128,2,128]{3,2,1,0:T(2,128)} copy(f32[4,128,2,128]{1,3,2,0:T(8,128)} %get-tuple-element.134) | data formatting | bytes 1048576 | tf_op jit(solution)/shard_map/add | solution.py:195
  146.2 2.8 %fusion.54 = bf16[512,256]{1,0:T(8,128)(2,1)} fusion(f32[64,8,2,128]{3,2,1,0:T(2,128)S(1)} %bitcast.175, f32[64,8,2,128]{3,2,1,0:T(2,128)} %bitcast.176, f32[256]{0:T(256)S(1)} %broadcast_bitcast_fusion, bf16[512,2048]{1,0:T(8,128)(2,1)S(1)} %copy-done.2, bf16[2048,256]{1,0:T(8,128)(2,1)} %param.21), kind=kOutput, calls=%fused_computation.76 | convolution fusion | flops 537919488 | bytes 4457472 | tf_op jit(solution)/shard_map/dot_general | solution.py:126
  149.0 1.5 copy.106
  150.5 22.6 %all_to_all.19 = bf16[256,4,512]{0,2,1:T(8,128)(2,1)S(1)} all-to-all(bf16[256,4,512]{0,2,1:T(8,128)(2,1)S(1)} %bitcast.172), channel_id=1, replica_groups=mesh['seq'=8,'head'=4] {'head'}, dimensions={1} | all-to-all | bytes 2097152 | tf_op jit(solution)/shard_map/all_to_all | solution.py:206
  173.6 2.7 %convolution_convert_fusion = bf16[512,512]{1,0:T(8,128)(2,1)} fusion(bf16[512,1024]{1,0:T(8,128)(2,1)} %all-gather.7.cloned.1.call-done, bf16[1024,512]{1,0:T(8,128)(2,1)S(1)} %bitcast.174), kind=kOutput, calls=%fused_computation.17 | convolution fusion | flops 537133056 | bytes 2621440 | tf_op jit(solution)/shard_map/dot_general | solution.py:207
  (144 shorter events, 34.6 us)
Async XLA Ops:
  6.5 31.6 %copy-start = (bf16[2048,256]{1,0:T(8,128)(2,1)S(1)}, bf16[2048,256]{1,0:T(8,128)(2,1)}, u32[]{:S(2)}) copy-start(bf16[2048,256]{1,0:T(8,128)(2,1)} %param.20) | copy-start | bytes 3145732
  6.5 27.7 %all-gather.5.cloned.1.call-start = ((), (), s32[]{:S(2)}) async-start(), calls=%async_computation.1 | async-start | bytes 2621440 | tf_op jit(solution)/shard_map/all_gather | solution.py:124
  7.3 120.7 %all-gather.9.cloned.1.call-start = ((), (), s32[]{:S(2)}) async-start(), calls=%async_computation.3 | async-start | bytes 2359296 | tf_op jit(solution)/shard_map/all_gather | solution.py:173
  34.2 3.9 %copy-start.1 = (bf16[512,2048]{1,0:T(8,128)(2,1)S(1)}, bf16[512,2048]{1,0:T(8,128)(2,1)}, u32[]{:S(2)}) copy-start(bf16[512,2048]{1,0:T(8,128)(2,1)} %all-gather.5.cloned.1.call-done) | copy-start | bytes 6291460
  38.2 1.2 copy-start.16
  38.9 2.8 %copy-start.3 = (f32[512,256]{1,0:T(8,128)}, f32[512,256]{1,0:T(8,128)S(1)}, u32[]{:S(2)}) copy-start(f32[512,256]{1,0:T(8,128)S(1)} %fusion.152) | copy-start | bytes 1572868
  38.9 2.0 %copy-start.17 = (bf16[2048,256]{1,0:T(8,128)(2,1)S(1)}, bf16[2048,256]{1,0:T(8,128)(2,1)}, u32[]{:S(2)}) copy-start(bf16[2048,256]{1,0:T(8,128)(2,1)} %param.18) | copy-start | bytes 3145732
  40.1 0.8 copy-start.7
  40.9 4.3 %copy-start.8 = (bf16[2048,2]{0,1:T(2,128)(2,1)S(1)}, bf16[2048,2]{0,1:T(2,128)(2,1)}, u32[]{:S(2)}) copy-start(bf16[2048,2]{0,1:T(2,128)(2,1)} %param.22) | copy-start | bytes 24580
  40.9 4.4 %copy-start.15 = (f32[2]{0:T(128)S(1)}, f32[2]{0:T(128)}, u32[]{:S(2)}) copy-start(f32[2]{0:T(128)} %param.26) | copy-start | bytes 28
  41.7 4.3 %copy-start.5 = (f32[512,256]{1,0:T(8,128)}, f32[512,256]{1,0:T(8,128)S(1)}, u32[]{:S(2)}) copy-start(f32[512,256]{1,0:T(8,128)S(1)} %fusion.150) | copy-start | bytes 1572868
  41.7 4.8 %collective-permute-start = (f32[3,768]{1,0:T(4,128)S(1)}, f32[3,768]{1,0:T(4,128)S(1)}, u32[]{:S(2)}, u32[]{:S(2)}) collective-permute-start(f32[3,768]{1,0:T(4,128)S(1)} %pad_maximum_fusion.4), channel_id=1, source_target_pairs={{0,4},{4,8},{8,12},{12,16},{16,20},{20,24},{24,28},{1,5},{5,9},{9,... | collective-permute-start | bytes 27656 | tf_op jit(solution)/shard_map/ppermute | solution.py:14
  59.6 3.5 %copy-start.4 = (f32[512,256]{1,0:T(8,128)S(1)}, f32[512,256]{1,0:T(8,128)}, u32[]{:S(2)}) copy-start(f32[512,256]{1,0:T(8,128)} %copy-done.3) | copy-start | bytes 1572868
  59.6 3.5 %copy-start.6 = (f32[512,256]{1,0:T(8,128)S(1)}, f32[512,256]{1,0:T(8,128)}, u32[]{:S(2)}) copy-start(f32[512,256]{1,0:T(8,128)} %copy-done.5) | copy-start | bytes 1572868
  59.6 3.5 %copy-start.9 = (f32[1,1,256]{2,0,1:T(1,128)S(1)}, f32[1,1,256]{2,0,1:T(1,128)}, u32[]{:S(2)}) copy-start(f32[1,1,256]{2,0,1:T(1,128)} %get-tuple-element.113) | copy-start | bytes 3076
  59.6 3.5 %copy-start.10 = (f32[1,1,256]{2,0,1:T(1,128)S(1)}, f32[1,1,256]{2,0,1:T(1,128)}, u32[]{:S(2)}) copy-start(f32[1,1,256]{2,0,1:T(1,128)} %get-tuple-element.114) | copy-start | bytes 3076
  59.6 3.5 %copy-start.11 = (f32[1,1,256]{2,0,1:T(1,128)S(1)}, f32[1,1,256]{2,0,1:T(1,128)}, u32[]{:S(2)}) copy-start(f32[1,1,256]{2,0,1:T(1,128)} %get-tuple-element.115) | copy-start | bytes 3076
  59.6 3.5 %copy-start.12 = (f32[1,1,256]{2,0,1:T(1,128)S(1)}, f32[1,1,256]{2,0,1:T(1,128)}, u32[]{:S(2)}) copy-start(f32[1,1,256]{2,0,1:T(1,128)} %get-tuple-element.116) | copy-start | bytes 3076
  59.6 3.5 %copy-start.13 = (f32[1,1,256]{2,0,1:T(1,128)S(1)}, f32[1,1,256]{2,0,1:T(1,128)}, u32[]{:S(2)}) copy-start(f32[1,1,256]{2,0,1:T(1,128)} %get-tuple-element.117) | copy-start | bytes 3076
  59.6 3.5 %copy-start.14 = (f32[1,1,256]{2,0,1:T(1,128)S(1)}, f32[1,1,256]{2,0,1:T(1,128)}, u32[]{:S(2)}) copy-start(f32[1,1,256]{2,0,1:T(1,128)} %get-tuple-element.118) | copy-start | bytes 3076
  71.0 6.9 %copy-start.18 = (f32[128]{0:T(128)S(1)}, f32[128]{0:T(128)}, u32[]{:S(2)}) copy-start(f32[128]{0:T(128)} %param.28) | copy-start | bytes 1540
  77.8 95.8 %all-gather.7.cloned.1.call-start = ((), (), s32[]{:S(2)}) async-start(), calls=%async_computation.2 | async-start | bytes 1310720 | tf_op jit(solution)/shard_map/all_gather | solution.py:208
  139.5 6.6 %copy-start.2 = (bf16[512,2048]{1,0:T(8,128)(2,1)S(1)}, bf16[512,2048]{1,0:T(8,128)(2,1)}, u32[]{:S(2)}) copy-start(bf16[512,2048]{1,0:T(8,128)(2,1)} %all-gather.5.cloned.1.call-done) | copy-start | bytes 6291460
Sparse Core Ops, SparseCore 0:
  8.9 25.2 all-gather.4
  78.0 49.9 all-gather.8
  149.1 21.0 all-gather.6
where the time goes:
time: 184 us; the launch traced here: 183 us
  waiting for transfers between devices  59.6 us (32%)
  matrix products  49.9 us (27%)
  blocking collectives  22.6 us (12%)
  local copies, waits for them, and re-layouts  17.1 us (9%)
  other arithmetic  15.9 us (9%)
  between operations  13.9 us (8%)
  starting transfers between devices  3.64 us (2%)
    all_gather x1, waiting for transfers between devices, on_device(): every_map = lax.all_gather(stacked, 'seq', axis=0, tiled=True)  35 us
    all_gather x1, waiting for transfers between devices, on_device(): shard_piece = lax.all_gather(layer_in, 'head', axis=1, tiled=True)  23.5 us
    all_to_all x1, blocking collectives, on_device(): lax.all_to_all(out_weight, 'head', split_axis=1, concat_axis=0, tiled=True)  22.6 us
    dot_general x6, matrix products, on_device(): jnp.dot(shard_piece, weight, preferred_element_type=jnp.float32)  8.02 us
    dot_general x7, matrix products, compose(): jnp.einsum('...de,...ef->...df', later_map[0], earlier[1], precision=exac...  6.03 us
    dot_general x7, matrix products, unit_lower_inverse(): jnp.einsum('...rs,...st->...rt', inverse, middle, precision=exact_mode)  5.27 us
    dot_general x7, matrix products, unit_lower_inverse(): jnp.einsum('...rs,...st->...rt', linking, inverse, precision=exact_mode)  4.78 us
    dot_general x4, matrix products, advance(): jnp.einsum('hde,hef->hdf', block_maps[0], carry_state, precision=exact_mode)  4.67 us
  transfers between devices with their start and end apart: 4, of which 3 were waited for; matrix products, arithmetic and copies ran while one was open for 12% of the time, Pallas kernels for 0%

commit v1 on v0

--- a/solution.py
+++ b/solution.py
@@ -121,7 +121,7 @@
     head_count = beta_weight.shape[1]
     head_dim = query_weight.shape[1] // head_count
     weights = (query_weight, key_weight, value_weight, gate_weight, beta_weight, decay_weight)
-    shard_piece = lax.all_gather(layer_in, "head", axis=1, tiled=True)
+    shard_piece = jnp.concatenate(lax.all_gather(layer_in, "head"), axis=1)
     query_raw, key_raw, value_raw, gate_raw, beta_raw, decay_raw = tuple(
         (jnp.dot(shard_piece, weight, preferred_element_type=jnp.float32) for weight in weights)
     )

time: 184 us -> 204 us (1.11)
  local copies, waits for them, and re-layouts: 17.1 us -> 33.1 us
  other arithmetic: 15.9 us -> 22.2 us
  waiting for transfers between devices: 59.6 us -> 54.4 us
  matrix products: 49.9 us -> 52.6 us
    all_gather x1, waiting for transfers between devices: 35 us -> 30.2 us  [on_device(): every_map = lax.all_gather(stacked, 'seq', axis=0, tiled=True)]
    reshape x0 -> x2, local copies, waits for them, and re-layouts: none -> 4.8 us  [the longest x1 2.76 us: on_device(): shard_piece = jnp.concatenate(lax.all_gather(layer_in, 'head'), axis=1)]
    dot_general x5, matrix products: 1.73 us -> 5.35 us  [compose(): jnp.einsum('...de,...ef->...df', later_map[0], earlier[0], precision=exac...]
    all_gather x0 -> x1, local copies, waits for them, and re-layouts: none -> 3.21 us  [on_device(): shard_piece = jnp.concatenate(lax.all_gather(layer_in, 'head'), axis=1)]
    unnamed x41 -> x70, local copies, waits for them, and re-layouts: 4 us -> 7.1 us
    dot_general x0 -> x1, local copies, waits for them, and re-layouts: none -> 2.29 us  [on_device(): jnp.dot(shard_piece, weight, preferred_element_type=jnp.float32)]
  transfers between devices with their start and end apart: 4 -> 4, of which waited for: 3 -> 2; matrix products, arithmetic and copies ran while one was open for 12% -> 14% of each run, Pallas kernels for 0% -> 0%
where the time goes in v1:
time: 204 us; the launch traced here: 203 us
  waiting for transfers between devices  54.4 us (27%)
  matrix products  52.6 us (26%)
  local copies, waits for them, and re-layouts  33.1 us (16%)
  blocking collectives  22.6 us (11%)
  other arithmetic  22.2 us (11%)
  between operations  14 us (7%)
  starting transfers between devices  3.45 us (2%)
    all_gather x1, waiting for transfers between devices, on_device(): every_map = lax.all_gather(stacked, 'seq', axis=0, tiled=True)  30.2 us
    all_gather x1, waiting for transfers between devices, on_device(): shard_piece = jnp.concatenate(lax.all_gather(layer_in, 'head'), axis=1)  23.4 us
    all_to_all x1, blocking collectives, on_device(): lax.all_to_all(out_weight, 'head', split_axis=1, concat_axis=0, tiled=True)  22.6 us
    dot_general x6, matrix products, on_device(): jnp.dot(shard_piece, weight, preferred_element_type=jnp.float32)  8.01 us
    unnamed x70, local copies, waits for them, and re-layouts  7.1 us
    dot_general x7, matrix products, compose(): jnp.einsum('...de,...ef->...df', later_map[0], earlier[1], precision=exac...  6.29 us
    dot_general x5, matrix products, compose(): jnp.einsum('...de,...ef->...df', later_map[0], earlier[0], precision=exac...  5.35 us
    dot_general x7, matrix products, unit_lower_inverse(): jnp.einsum('...rs,...st->...rt', inverse, middle, precision=exact_mode)  5.27 us
  transfers between devices with their start and end apart: 4, of which 2 were waited for; matrix products, arithmetic and copies ran while one was open for 14% of the time, Pallas kernels for 0%

profile of v1, /device:TPU:0, one launch (start us, length us, event | category | flops | bytes accessed | tf_op | source)
XLA Modules:
  0.0 202.5 jit_solution(17918753465601762728)
XLA Ops:
  8.7 1.5 fusion.145
  10.8 23.4 %all-gather.8.cloned.1.call-done = bf16[2048,512]{1,0:T(8,128)(2,1)} async-done(((bf16[512,512]{1,0:T(8,128)(2,1)}), bf16[2048,512]{1,0:T(8,128)(2,1)}) %all-gather.8.cloned.1.call-update) | async-done | bytes 2097168 | tf_op jit(solution)/shard_map/all_gather | solution.py:124
  34.2 3.2 %copy.123 = bf16[4,512,512]{2,0,1:T(4,128)(2,1)S(1)} copy(bf16[4,512,512]{2,1,0:T(8,128)(2,1)} %bitcast.174) | data formatting | bytes 4194304 | tf_op jit(solution)/shard_map/all_gather | solution.py:124
  43.2 3.4 %collective-permute-start = (f32[3,768]{1,0:T(4,128)S(1)}, f32[3,768]{1,0:T(4,128)S(1)}, u32[]{:S(2)}, u32[]{:S(2)}) collective-permute-start(f32[3,768]{1,0:T(4,128)S(1)} %pad_maximum_fusion.4), channel_id=1, source_target_pairs={{0,4},{4,8},{8,12},{12,16},{16,20},{20,24},{24,28},{1,5},{5,9},{9,... | collective-permute-start | bytes 27656 | tf_op jit(solution)/shard_map/ppermute | solution.py:14
  48.9 2.3 %fusion.147 = (f32[4,2,128]{2,1,0:T(2,128)S(1)}, f32[4,2,128]{2,1,0:T(2,128)S(1)}, f32[4,2,128]{2,1,0:T(2,128)S(1)}, f32[4,2,128]{2,1,0:T(2,128)S(1)}) fusion(f32[4,2,128]{2,1,0:T(2,128)S(1)} %reduce_window_sum.11, f32[4,2]{1,0:T(4,128)S(1)} %copy.78, f32[2]{0:T(128)S(1)} %copy-done.28, bf16[512,2048]{1,0:T(8,128)(2,1)} %bitcast.169, ...), kind=kOutput, calls=%fused_computation.242 | convolution fusion | flops 4200448 | bytes 2125864 | tf_op jit(solution)/shard_map/dot_general | solution.py:126
  51.3 3.0 %fusion.143 = (f32[512,256]{1,0:T(8,128)}, f32[512,256]{1,0:T(8,128)}) fusion(f32[512,256]{1,0:T(8,128)} %copy-done.16, f32[3,256]{1,0:T(4,128)S(1)} %get-tuple-element.122, f32[256]{0:T(256)} %bitcast.197, f32[256]{0:T(256)} %bitcast.198, f32[256]{0:T(256)} %bitcast.199, f32[256]{0:T(256)} %bitcast.200), kind=kLoop, calls=%fused_computation.238 | loop fusion | flops 1966080 | bytes 1580032 | tf_op jit(solution)/shard_map/mul | solution.py:30
  54.3 2.1 %mul.286 = f32[512,2,128]{2,1,0:T(2,128)} reshape(f32[512,256]{1,0:T(8,128)} %get-tuple-element.103) | data formatting | bytes 1048576 | tf_op jit(solution)/shard_map/mul | solution.py:30
  56.4 2.4 %reduce_sum.28 = f32[512,2]{1,0:T(8,128)} reduce(f32[512,2,128]{2,1,0:T(2,128)} %mul.286, f32[]{:T(128)} %constant.223.clone.1), dimensions={2}, to_apply=%region_2.3 | reduce | flops 130048 | bytes 528388 | tf_op jit(solution)/shard_map/reduce_sum | solution.py:30
  58.8 1.7 add_rsqrt_fusion
  61.6 2.1 %reshape.148 = f32[4,128,2,128]{3,2,1,0:T(2,128)} reshape(f32[512,256]{1,0:T(8,128)} %get-tuple-element.104) | data formatting | bytes 1048576 | tf_op jit(solution)/shard_map/reshape | solution.py:143
  63.7 2.6 %fusion.16 = f32[4,2,128,128]{3,2,1,0:T(8,128)S(1)} fusion(f32[4,128,2,128]{3,2,1,0:T(2,128)} %reshape.148, f32[4,2,128]{2,1,0:T(2,128)S(1)} %get-tuple-element.134, f32[128,128]{1,0:T(8,128)S(1)} %fusion.130, f32[4,128,2]{1,2,0:T(2,128)S(1)} %bitcast.181, f32[4,2,128]{2,1,0:T(2,128)S(1)} %reduce_window_sum.11, ...), kind=kOutput, calls=%fused_computation.23 | convolution fusion | flops 202375168 | bytes 1159168 | tf_op jit(solution)/shard_map/...rd,...sd->...rs/dot_general | solution.py:63
  78.2 1.5 fusion.142
  79.6 2.1 %reshape_reshape.3 = f32[4,128,2,128]{3,2,1,0:T(2,128)} reshape(f32[512,256]{1,0:T(8,128)} %get-tuple-element.137) | data formatting | bytes 1048576 | tf_op jit(solution)/shard_map/reshape;reshape | solution.py:150
  83.1 2.4 %fusion.27 = f32[4,2,128,256]{3,2,1,0:T(8,128)S(1)} fusion(f32[4,2,128,128]{3,2,1,0:T(8,128)} %bitcast_multiply_fusion.2, f32[4,2,128,128]{3,2,1,0:T(8,128)S(1)} %bitcast_multiply_fusion, f32[4,2,128,128]{3,2,1,0:T(8,128)} %copy-done.7, f32[4,2,128,128]{3,2,1,0:T(8,128)} %fusion.155), kind=kOutput, calls=%fused_computation.42 | convolution fusion | flops 403046400 | bytes 3145728 | tf_op jit(solution)/shard_map/...rs,...se->...re/dot_general | solution.py:70
  85.5 2.1 %fusion.78 = f32[4,2,128,128]{3,2,1,0:T(8,128)} fusion(f32[4,2,128,256]{3,2,1,0:T(8,128)S(1)} %fusion.27, f32[4,128,2,128]{3,2,1,0:T(2,128)S(1)} %copy-done.5, f32[4,2,128]{2,1,0:T(2,128)S(1)} %get-tuple-element.126, f32[4,128,2]{1,2,0:T(2,128)S(1)} %bitcast.183), kind=kOutput, calls=%fused_computation.114 | convolution fusion | flops 201588736 | bytes 1581056 | tf_op jit(solution)/shard_map/...bd,...be->...de/dot_general | solution.py:92
  89.8 9.9 %while.28 = (s32[]{:T(128)}, f32[2,128,128]{2,1,0:T(8,128)S(1)}, f32[2,128,128]{2,1,0:T(8,128)S(1)}, f32[4,2,128,128]{3,2,1,0:T(8,128)}, f32[4,2,128,128]{3,2,1,0:T(8,128)}) while((s32[]{:T(128)}, f32[2,128,128]{2,1,0:T(8,128)S(1)}, f32[2,128,128]{2,1,0:T(8,128)S(1)}, f32[4,2,128,128]{3,2,1,0:T(8,128)}, ...), condition=%wide.region_4.5_spmd.clone.clone, body=%wide.region_3.4_spmd.clone.sunk.clone | while | flops 100728832 | bytes 1443399 | solution.py:170
  100.6 2.3 %copy.90 = bf16[256,2048]{1,0:T(8,128)(2,1)} copy(bf16[256,2048]{0,1:T(8,128)(2,1)} %bitcast.177) | data formatting | bytes 2097152 | tf_op jit(solution)/shard_map/dot_general | solution.py:126
  102.9 2.8 %reshape.155 = bf16[512,2048,1]{1,0,2:T(8,128)(2,1)} reshape(bf16[512,4,512]{2,1,0:T(4,128)(2,1)S(1)} %bitcast.164) | data formatting | bytes 4194304 | tf_op jit(solution)/shard_map/reshape | solution.py:124
  105.7 2.2 %mul.269 = f32[512,2,128]{2,1,0:T(2,128)} reshape(f32[512,256]{1,0:T(8,128)} %get-tuple-element.101) | data formatting | bytes 1048576 | tf_op jit(solution)/shard_map/mul | solution.py:30
  107.8 2.5 %reduce_sum.27 = f32[512,2]{1,0:T(8,128)} reduce(f32[512,2,128]{2,1,0:T(2,128)} %mul.269, f32[]{:T(128)} %constant.223.clone.1), dimensions={2}, to_apply=%region_1.2 | reduce | flops 130048 | bytes 528388 | tf_op jit(solution)/shard_map/reduce_sum | solution.py:30
  110.4 1.7 add_rsqrt_fusion.1
  114.2 2.4 %fusion.17 = f32[4,2,128,128]{3,2,1,0:T(8,128)S(1)} fusion(f32[4,128,2,128]{3,2,1,0:T(2,128)} %reshape.147, f32[4,128,2,128]{3,2,1,0:T(2,128)S(1)} %copy-done.6, f32[4,128,2]{1,2,0:T(2,128)S(1)} %bitcast.185, f32[4,128,2]{1,2,0:T(2,128)S(1)} %bitcast.186, f32[4,2,128]{2,1,0:T(2,128)S(1)} %reduce_window_sum.11, pred[128,128]{1,0:T(8,128)(4,1)S(1)} %get-tuple-element.139), kind=kOutput, calls=%fused_computation.25 | convolution fusion | flops 202244096 | bytes 1601536 | tf_op jit(solution)/shard_map/...rd,...sd->...rs/dot_general | solution.py:76
  117.2 1.5 fusion.84
  118.7 30.2 %all-gather.10.cloned.1.call-done = f32[16,2,128,128]{3,2,1,0:T(8,128)} async-done(((f32[2,2,128,128]{3,2,1,0:T(8,128)}), f32[16,2,128,128]{3,2,1,0:T(8,128)}) %all-gather.10.cloned.1.call-update) | async-done | bytes 2097168 | tf_op jit(solution)/shard_map/all_gather | solution.py:173
  148.9 1.8 fusion.25
  152.9 7.8 %while.27 = (s32[]{:T(128)}, f32[2,128,128]{2,1,0:T(8,128)S(1)}, f32[4,2,128,128]{3,2,1,0:T(8,128)}, f32[4,2,128,128]{3,2,1,0:T(8,128)}, f32[4,2,128,128]{3,2,1,0:T(8,128)}) while((s32[]{:T(128)}, f32[2,128,128]{2,1,0:T(8,128)S(1)}, f32[4,2,128,128]{3,2,1,0:T(8,128)}, f32[4,2,128,128]{3,2,1,0:T(8,128)}, ...), condition=%wide.region_6.7_spmd.clone, body=%wide.region_5.6_spmd.sunk.clone | while | flops 50364416 | bytes 1050173 | solution.py:194
  160.7 2.0 multiply_reduce_fusion
  163.6 2.0 %copy.84 = f32[512,2,128]{0,2,1:T(8,128)} copy(f32[512,2,128]{2,0,1:T(8,128)} %bitcast.176) | data formatting | bytes 1048576 | tf_op jit(solution)/shard_map/reshape | solution.py:196
  165.7 2.9 %multiply_convert_fusion = bf16[512,2,128]{0,2,1:T(8,128)(2,1)} fusion(bf16[512,2048,1]{1,0,2:T(8,128)(2,1)S(1)} %copy-done.11, bf16[2,128,2048]{2,1,0:T(8,128)(2,1)} %bitcast.178, f32[512,2,128]{0,2,1:T(8,128)} %copy.84, f32[128]{0:T(128)S(1)} %copy-done.32, f32[512,2]{0,1:T(2,128)S(1)} %rsqrt_bitcast_fusion), kind=kOutput, calls=%fused_computation.89 | convolution fusion | flops 537919488 | bytes 3936768 | tf_op jit(solution)/shard_map/dot_general | solution.py:126
  168.6 1.5 copy.86
  170.1 22.6 %all_to_all.19 = bf16[256,4,512]{0,2,1:T(8,128)(2,1)S(1)} all-to-all(bf16[256,4,512]{0,2,1:T(8,128)(2,1)S(1)} %bitcast.173), channel_id=1, replica_groups=mesh['seq'=8,'head'=4] {'head'}, dimensions={1} | all-to-all | bytes 2097152 | tf_op jit(solution)/shard_map/all_to_all | solution.py:206
  193.2 2.8 %convolution_convert_fusion = bf16[512,512]{1,0:T(8,128)(2,1)} fusion(bf16[512,1024]{0,1:T(8,128)(2,1)} %all-gather.6.cloned.1.call-done, bf16[1024,512]{1,0:T(8,128)(2,1)S(1)} %bitcast.179), kind=kOutput, calls=%fused_computation.17 | convolution fusion | flops 537133056 | bytes 2621440 | tf_op jit(solution)/shard_map/dot_general | solution.py:207
  (174 shorter events, 51.4 us)
Async XLA Ops:
  6.5 31.5 %copy-start = (bf16[2048,256]{1,0:T(8,128)(2,1)S(1)}, bf16[2048,256]{1,0:T(8,128)(2,1)}, u32[]{:S(2)}) copy-start(bf16[2048,256]{1,0:T(8,128)(2,1)} %param.18) | copy-start | bytes 3145732
  6.5 27.7 %all-gather.8.cloned.1.call-start = ((), (), s32[]{:S(2)}) async-start(), calls=%async_computation.2 | async-start | bytes 2621440 | tf_op jit(solution)/shard_map/all_gather | solution.py:124
  7.3 141.6 %all-gather.10.cloned.1.call-start = ((), (), s32[]{:S(2)}) async-start(), calls=%async_computation.3 | async-start | bytes 2359296 | tf_op jit(solution)/shard_map/all_gather | solution.py:173
  38.1 8.5 %copy-start.1 = (bf16[64,8,4,512]{3,1,2,0:T(8,128)(2,1)}, bf16[64,8,4,512]{3,1,2,0:T(8,128)(2,1)S(1)}, u32[]{:S(2)}) copy-start(bf16[64,8,4,512]{3,1,2,0:T(8,128)(2,1)S(1)} %copy.93) | copy-start | bytes 6291460
  38.8 3.5 %copy-start.12 = (f32[512,256]{1,0:T(8,128)}, f32[512,256]{1,0:T(8,128)S(1)}, u32[]{:S(2)}) copy-start(f32[512,256]{1,0:T(8,128)S(1)} %fusion.148) | copy-start | bytes 1572868
  41.6 5.0 %copy-start.17 = (bf16[2048,2]{0,1:T(2,128)(2,1)S(1)}, bf16[2048,2]{0,1:T(2,128)(2,1)}, u32[]{:S(2)}) copy-start(bf16[2048,2]{0,1:T(2,128)(2,1)} %param.23) | copy-start | bytes 24580
  41.6 5.0 %copy-start.27 = (f32[2]{0:T(128)S(1)}, f32[2]{0:T(128)}, u32[]{:S(2)}) copy-start(f32[2]{0:T(128)} %param.27) | copy-start | bytes 28
  41.6 5.0 %copy-start.29 = (f32[2]{0:T(128)S(1)}, f32[2]{0:T(128)}, u32[]{:S(2)}) copy-start(f32[2]{0:T(128)} %exponential_negate_fusion) | copy-start | bytes 28
  41.6 7.3 %copy-start.18 = (bf16[2048,2]{0,1:T(2,128)(2,1)S(1)}, bf16[2048,2]{0,1:T(2,128)(2,1)}, u32[]{:S(2)}) copy-start(bf16[2048,2]{0,1:T(2,128)(2,1)} %param.22) | copy-start | bytes 24580
  41.6 7.3 %copy-start.28 = (f32[2]{0:T(128)S(1)}, f32[2]{0:T(128)}, u32[]{:S(2)}) copy-start(f32[2]{0:T(128)} %param.26) | copy-start | bytes 28
  43.2 8.1 %collective-permute-start = (f32[3,768]{1,0:T(4,128)S(1)}, f32[3,768]{1,0:T(4,128)S(1)}, u32[]{:S(2)}, u32[]{:S(2)}) collective-permute-start(f32[3,768]{1,0:T(4,128)S(1)} %pad_maximum_fusion.4), channel_id=1, source_target_pairs={{0,4},{4,8},{8,12},{12,16},{16,20},{20,24},{24,28},{1,5},{5,9},{9,... | collective-permute-start | bytes 27656 | tf_op jit(solution)/shard_map/ppermute | solution.py:14
  74.5 3.6 %copy-start.7 = (f32[4,2,128,128]{3,2,1,0:T(8,128)}, f32[4,2,128,128]{3,2,1,0:T(8,128)S(1)}, u32[]{:S(2)}) copy-start(f32[4,2,128,128]{3,2,1,0:T(8,128)S(1)} %sub.166) | copy-start | bytes 1572868
  74.5 3.6 %copy-start.13 = (f32[512,256]{1,0:T(8,128)S(1)}, f32[512,256]{1,0:T(8,128)}, u32[]{:S(2)}) copy-start(f32[512,256]{1,0:T(8,128)} %copy-done.12) | copy-start | bytes 1572868
  74.5 3.6 %copy-start.15 = (f32[512,256]{1,0:T(8,128)S(1)}, f32[512,256]{1,0:T(8,128)}, u32[]{:S(2)}) copy-start(f32[512,256]{1,0:T(8,128)} %copy-done.14) | copy-start | bytes 1572868
  74.5 3.6 %copy-start.19 = (f32[1,1,256]{2,0,1:T(1,128)S(1)}, f32[1,1,256]{2,0,1:T(1,128)}, u32[]{:S(2)}) copy-start(f32[1,1,256]{2,0,1:T(1,128)} %get-tuple-element.109) | copy-start | bytes 3076
  74.5 3.6 %copy-start.20 = (f32[1,1,256]{2,0,1:T(1,128)S(1)}, f32[1,1,256]{2,0,1:T(1,128)}, u32[]{:S(2)}) copy-start(f32[1,1,256]{2,0,1:T(1,128)} %get-tuple-element.110) | copy-start | bytes 3076
  74.5 3.6 %copy-start.21 = (f32[1,1,256]{2,0,1:T(1,128)S(1)}, f32[1,1,256]{2,0,1:T(1,128)}, u32[]{:S(2)}) copy-start(f32[1,1,256]{2,0,1:T(1,128)} %get-tuple-element.115) | copy-start | bytes 3076
  74.5 3.6 %copy-start.22 = (f32[1,1,256]{2,0,1:T(1,128)S(1)}, f32[1,1,256]{2,0,1:T(1,128)}, u32[]{:S(2)}) copy-start(f32[1,1,256]{2,0,1:T(1,128)} %get-tuple-element.116) | copy-start | bytes 3076
  74.5 3.6 %copy-start.23 = (f32[1,1,256]{2,0,1:T(1,128)S(1)}, f32[1,1,256]{2,0,1:T(1,128)}, u32[]{:S(2)}) copy-start(f32[1,1,256]{2,0,1:T(1,128)} %get-tuple-element.117) | copy-start | bytes 3076
  74.5 3.6 %copy-start.24 = (f32[1,1,256]{2,0,1:T(1,128)S(1)}, f32[1,1,256]{2,0,1:T(1,128)}, u32[]{:S(2)}) copy-start(f32[1,1,256]{2,0,1:T(1,128)} %get-tuple-element.118) | copy-start | bytes 3076
  74.6 3.6 %copy-start.25 = (f32[1,1,256]{2,0,1:T(1,128)S(1)}, f32[1,1,256]{2,0,1:T(1,128)}, u32[]{:S(2)}) copy-start(f32[1,1,256]{2,0,1:T(1,128)} %get-tuple-element.119) | copy-start | bytes 3076
  74.6 3.6 %copy-start.26 = (f32[1,1,256]{2,0,1:T(1,128)S(1)}, f32[1,1,256]{2,0,1:T(1,128)}, u32[]{:S(2)}) copy-start(f32[1,1,256]{2,0,1:T(1,128)} %get-tuple-element.120) | copy-start | bytes 3076
  81.8 3.7 %copy-start.5 = (f32[4,128,2,128]{3,2,1,0:T(2,128)S(1)}, f32[4,128,2,128]{3,2,1,0:T(2,128)}, u32[]{:S(2)}) copy-start(f32[4,128,2,128]{3,2,1,0:T(2,128)} %reshape.148) | copy-start | bytes 1572868
  85.5 4.4 %copy-start.2 = (f32[4,2,128,256]{3,2,1,0:T(8,128)}, f32[4,2,128,256]{3,2,1,0:T(8,128)S(1)}, u32[]{:S(2)}) copy-start(f32[4,2,128,256]{3,2,1,0:T(8,128)S(1)} %fusion.27) | copy-start | bytes 3145732
  100.5 92.7 %all-gather.6.cloned.1.call-start = ((), (), s32[]{:S(2)}) async-start(), calls=%async_computation.1 | async-start | bytes 1310720 | tf_op jit(solution)/shard_map/all_gather | solution.py:208
  105.6 7.5 %copy-start.9 = (f32[512,256]{1,0:T(8,128)S(1)}, f32[512,256]{1,0:T(8,128)}, u32[]{:S(2)}) copy-start(f32[512,256]{1,0:T(8,128)} %get-tuple-element.102) | copy-start | bytes 1572868
  105.6 8.5 %copy-start.6 = (f32[4,128,2,128]{3,2,1,0:T(2,128)S(1)}, f32[4,128,2,128]{3,2,1,0:T(2,128)}, u32[]{:S(2)}) copy-start(f32[4,128,2,128]{3,2,1,0:T(2,128)} %reshape.148) | copy-start | bytes 1572868
  107.8 8.7 %copy-start.3 = (f32[4,2,128,256]{3,2,1,0:T(8,128)S(1)}, f32[4,2,128,256]{3,2,1,0:T(8,128)}, u32[]{:S(2)}) copy-start(f32[4,2,128,256]{3,2,1,0:T(8,128)} %copy-done.2) | copy-start | bytes 3145732
  152.9 7.8 %copy-start.8 = (f32[4,2,128,128]{3,2,1,0:T(8,128)S(1)}, f32[4,2,128,128]{3,2,1,0:T(8,128)}, u32[]{:S(2)}) copy-start(f32[4,2,128,128]{3,2,1,0:T(8,128)} %fusion.84) | copy-start | bytes 1572868
  152.9 7.8 %copy-start.10 = (f32[4,128,2,128]{3,2,1,0:T(2,128)S(1)}, f32[4,128,2,128]{3,2,1,0:T(2,128)}, u32[]{:S(2)}) copy-start(f32[4,128,2,128]{3,2,1,0:T(2,128)} %reshape.147) | copy-start | bytes 1572868
  160.7 4.9 %copy-start.32 = (f32[128]{0:T(128)S(1)}, f32[128]{0:T(128)}, u32[]{:S(2)}) copy-start(f32[128]{0:T(128)} %param.28) | copy-start | bytes 1540
  162.8 2.9 %copy-start.11 = (bf16[512,2048,1]{1,0,2:T(8,128)(2,1)S(1)}, bf16[512,2048,1]{1,0,2:T(8,128)(2,1)}, u32[]{:S(2)}) copy-start(bf16[512,2048,1]{1,0,2:T(8,128)(2,1)} %reshape.155) | copy-start | bytes 6291460
  (5 other events, 8.9 us)
Sparse Core Ops, SparseCore 0:
  8.9 25.2 all-gather.7
  100.6 48.1 all-gather.9
  168.7 20.9 all-gather.5
